TPU v7x, 32 devices: a whole 2x2x4 slice. The times are simulated.
32 devices in a mesh: rel: 4 (over x, core), dst: 4 (over z), mp: 2 (over y).
Axes of the slice: x: 2, y: 2, z: 4, core: 2. Of those that a mesh axis runs over, the one named last changes fastest.
Arguments:
- node_table: bfloat16 [16384, 512], P(('rel', 'dst')), may hold values from -6 to 6
- edge_weights: bfloat16 [4, 32, 128, 128], P('rel', 'dst'), may hold values from -0.5 to 0.5
- src_ids: int32 [4, 32, 128], P('rel', 'dst'), may hold values from 0 to 1023
- dst_ids: int32 [4, 32, 128], P('rel', 'dst'), may hold values from 0 to 511
- block_mask: int32 [4, 32], P('rel', 'dst'), may hold values 0 or 1
- basis_coef: float32 [4, 32], P('rel'), may hold values from -0.375 to 0.375
- basis_mats: bfloat16 [32, 512, 512], P(None, None, 'mp'), may hold values from -0.25 to 0.25
- type_bias: float32 [4, 512], P(None, 'mp'), may hold values from -3 to 3
- type_rows: int32 [4], replicated, may hold values from 1 to 256, 512 in all
- cotangent: bfloat16 [2048, 512], P(('rel', 'dst'), 'mp'), may hold values from -0.005859375 to 0.005859375
Outputs:
- layer_out: bfloat16 [2048, 512], P(('rel', 'dst'), 'mp')
- coef_grad: float32 [4, 32], P('rel')
Inputs may be any that keep to these rules, and one draw needn't show every extreme that they name: `type_rows`: the 4 counts sum to 512.
All inputs are finite; a program needn't handle non-finite values. No bound on the sum of `block_mask` on one device may be relied on, other than what follows from the above.
Results may differ from a plain program's by a relative error of at most 0.0062.
Values may be sent and summed in bfloat16 or wider, within the bound.
No kernel may reach another device: no remote copies, remote signals or barrier semaphores. Data moves between devices by JAX's collectives and lax.ppermute only.
A program may use at most 64 MiB of HBM per device.

v0:
```python
import jax
import jax.numpy as jnp
from jax import lax
from jax.sharding import PartitionSpec as P

highest = lax.Precision.HIGHEST


def on_device(
    node_table,
    edge_weights,
    src_ids,
    dst_ids,
    block_mask,
    basis_coef,
    basis_mats,
    type_bias,
    type_rows,
    cotangent,
):
    features = node_table.shape[1]
    out_cols = basis_mats.shape[2]
    basis_count = basis_mats.shape[0]
    block_count = edge_weights.shape[1]
    block_rows = edge_weights.shape[2]
    local_rows = cotangent.shape[0]
    owner_span = local_rows * lax.axis_size("rel")
    contract_rows = (((0,), (0,)), ((), ()))
    picked = jnp.take(node_table, src_ids[0].reshape(-1), axis=0).reshape(
        block_count, block_rows, features
    )
    scaled = edge_weights[0] * block_mask[0][:, None, None].astype(jnp.bfloat16)
    messages = jnp.einsum(
        "kij,kjf->kif", scaled, picked, preferred_element_type=jnp.float32
    ).astype(jnp.bfloat16)
    basis_flat = basis_mats.reshape(basis_count, -1)
    mixing = jnp.dot(basis_coef[0], basis_flat, precision=highest)
    weight = mixing.reshape(features, out_cols).astype(jnp.bfloat16)
    owner_grad = lax.all_gather(cotangent, "rel", axis=0, tiled=True)
    slot_local = dst_ids[0]
    arrived, arrived_ids = (
        lax.all_to_all(messages, "dst", split_axis=0, concat_axis=0, tiled=True),
        lax.all_to_all(slot_local, "dst", split_axis=0, concat_axis=0, tiled=True),
    )
    flat_rows = arrived.reshape(-1, features)
    outgoing = jnp.dot(flat_rows, weight, preferred_element_type=jnp.float32).astype(jnp.bfloat16)
    selector = (
        jnp.arange(owner_span, dtype=jnp.int32)[:, None] == arrived_ids.reshape(1, -1)
    ).astype(jnp.bfloat16)
    summed = jnp.dot(selector, outgoing, preferred_element_type=jnp.float32)
    wanted = lax.dot_general(
        selector, owner_grad, contract_rows, preferred_element_type=jnp.float32
    ).astype(jnp.bfloat16)
    outer_sum = lax.dot_general(
        flat_rows, wanted, contract_rows, preferred_element_type=jnp.float32
    )
    relation_total = lax.psum_scatter(summed, "rel", scatter_dimension=0, tiled=True)
    position = lax.axis_index("rel") * local_rows + jnp.arange(local_rows, dtype=jnp.int32)
    bounds = jnp.cumsum(type_rows)
    row_kind = jnp.sum((position[:, None] >= bounds[None, :]).astype(jnp.int32), axis=1)
    kind_table = (
        row_kind[:, None] == jnp.arange(type_rows.shape[0], dtype=jnp.int32)[None, :]
    ).astype(jnp.float32)
    row_bias = jnp.dot(kind_table, type_bias, precision=highest)
    layer_out = (relation_total + row_bias).astype(jnp.bfloat16)
    partial_value = jnp.dot(basis_flat, outer_sum.reshape(-1), precision=highest)
    basis_grads = lax.psum(partial_value, ("dst", "mp"))
    return (layer_out, basis_grads[None, :])


def solution(mesh):
    in_specs = (
        P(("rel", "dst"), None),
        P("rel", "dst", None, None),
        P("rel", "dst", None),
        P("rel", "dst", None),
        P("rel", "dst"),
        P("rel", None),
        P(None, None, "mp"),
        P(None, "mp"),
        P(),
        P(("rel", "dst"), "mp"),
    )
    out_specs = (P(("rel", "dst"), "mp"), P("rel", None))
    return jax.shard_map(
        on_device, mesh=mesh, in_specs=in_specs, out_specs=out_specs, check_vma=False
    )
```

profile of v0, /device:TPU:0, one launch (start us, length us, event | category | flops | bytes accessed | tf_op | source)
XLA Modules:
  0.0 98.5 jit_solution(5001905134119328474)
XLA Ops:
  7.2 0.0 copy-start
  7.2 0.0 copy-start.1
  7.2 0.0 copy-start.2
  7.2 0.0 copy-start.4
  7.2 6.5 %all-to-all-start = ((s32[4,2,128]{2,1,0:T(2,128)}), s32[4,2,128]{2,1,0:T(2,128)S(1)}, u32[]{:S(2)}, u32[]{:S(2)}) async-start(s32[4,2,128]{2,1,0:T(2,128)} %bitcast.52), calls=%async_computation | async-start | bytes 8192 | tf_op jit(solution)/shard_map/all_to_all | solution.py:43
  13.7 0.7 compare_and_fusion
  14.4 0.7 compare_select_fusion
  15.1 0.7 convert_bitcast_fusion
  15.8 0.0 copy-done
  15.8 4.0 %gather_fusion = bf16[1024,512]{1,0:T(8,128)(2,1)S(1)} fusion(bf16[1024,512]{1,0:T(8,128)(2,1)S(1)} %copy-done, s32[1024]{0:T(1024)S(1)} %broadcast_clamp_fusion), kind=kCustom, calls=%fused_computation | custom fusion | bytes 2101248 | tf_op jit(solution)/shard_map/jit(_take)/gather | solution.py:29
  19.7 0.0 copy-done.1
  19.7 1.5 %convolution_convert_fusion = bf16[8,128,512]{2,1,0:T(8,128)(2,1)} fusion(bf16[8,128,512]{2,1,0:T(8,128)(2,1)S(1)} %bitcast.47, pred[8,128]{1,0:T(8,128)(4,1)S(1)} %compare_and_fusion, bf16[1,8,128,128]{3,2,1,0:T(8,128)(2,1)S(1)} %copy-done.1, bf16[8]{0:T(256)(128)(2,1)S(1)} %convert_bitcast_fusion), kind=kOutput, calls=%fused_computation.9 | convolution fusion | flops 135397376 | bytes 2360336 | tf_op jit(solution)/shard_map/kij,kjf->kif/dot_general | solution.py:33
  21.2 0.0 all-to-all-done
  21.2 5.1 %all-to-all-start.1 = ((bf16[8,128,512]{2,1,0:T(8,128)(2,1)}), bf16[8,128,512]{2,1,0:T(8,128)(2,1)S(1)}, u32[]{:S(2)}, u32[]{:S(2)}) async-start(bf16[8,128,512]{2,1,0:T(8,128)(2,1)} %convolution_convert_fusion), calls=%async_computation.1 | async-start | bytes 2097152 | tf_op jit(solution)/shard_map/all_to_all | solution.py:42
  26.3 0.0 copy-start.5
  26.3 0.0 reduce-scatter.2.cloned.1.call-start
  26.3 0.0 copy-done.2
  26.3 5.8 %all_gather.3 = bf16[512,256]{1,0:T(8,128)(2,1)S(1)} all-gather(bf16[128,256]{1,0:T(8,128)(2,1)S(1)} %copy-done.2), channel_id=1, replica_groups=mesh['rel'=4,'dst'=4,'mp'=2] {'rel'}, dimensions={0}, use_global_device_ids=true | all-gather | bytes 327680 | tf_op jit(solution)/shard_map/all_gather | solution.py:39
  32.1 0.0 copy-done.4
  32.1 11.5 %fusion = bf16[1,512,256]{2,0,1:T(2,128)(2,1)S(1)} fusion(f32[1,32]{1,0:T(1,128)S(1)} %copy-done.4, bf16[4,8,512,256]{3,2,1,0:T(8,128)(2,1)} %bitcast.55), kind=kOutput, calls=%fused_computation.1 | convolution fusion | flops 50331648 | bytes 8650880 | tf_op jit(solution)/shard_map/dot_general | solution.py:37
  43.6 7.9 %all-to-all-done.1 = bf16[8,128,512]{2,1,0:T(8,128)(2,1)S(1)} async-done(((bf16[8,128,512]{2,1,0:T(8,128)(2,1)}), bf16[8,128,512]{2,1,0:T(8,128)(2,1)S(1)}, u32[]{:S(2)}, u32[]{:S(2)}) %all-to-all-start.1) | async-done | bytes 1048608 | tf_op jit(solution)/shard_map/all_to_all | solution.py:42
  51.5 0.0 copy-start.3
  51.5 1.9 %fusion.6 = f32[512,256]{1,0:T(8,128)} fusion(bf16[1024,512]{1,0:T(8,128)(2,1)S(1)} %bitcast.48, s32[1024]{0:T(1024)S(1)} %bitcast.53, bf16[1,512,256]{2,0,1:T(2,128)(2,1)S(1)} %fusion), kind=kOutput, calls=%fused_computation.8 | convolution fusion | flops 537657344 | bytes 1839104 | tf_op jit(solution)/shard_map/dot_general | solution.py:50
  53.4 0.0 reduce-scatter.2.cloned.1.call-update
  53.4 0.0 copy-done.5
  53.4 0.2 reduce-window.8
  53.6 0.1 convert_reduce_fusion
  53.7 1.2 %fusion.9 = f32[512,256,1]{1,0,2:T(8,128)S(1)} fusion(bf16[1024,512]{1,0:T(8,128)(2,1)S(1)} %bitcast.49, bf16[512,256]{1,0:T(8,128)(2,1)S(1)} %all_gather.3, s32[1024]{0:T(1024)S(1)} %bitcast.54), kind=kOutput, calls=%fused_computation.13 | convolution fusion | flops 537657344 | bytes 1839104 | tf_op jit(solution)/shard_map/dot_general | solution.py:54
  54.9 14.9 %fusion.11 = f32[1,32]{1,0:T(1,128)S(1)} fusion(bf16[32,512,256]{2,1,0:T(8,128)(2,1)} %param.16, f32[512,256,1]{1,0,2:T(8,128)S(1)} %fusion.9), kind=kOutput, calls=%fused_computation.16 | convolution fusion | flops 50331648 | bytes 8913024 | tf_op jit(solution)/shard_map/dot_general | solution.py:66
  69.8 20.0 %psum.7 = f32[1,32]{1,0:T(1,128)} all-reduce(f32[1,32]{1,0:T(1,128)S(1)} %fusion.11), channel_id=1, replica_groups=mesh['rel'=4,'dst'=4,'mp'=2] {'dst','mp'}, use_global_device_ids=true, to_apply=%region_3.4 | all-reduce | flops 32 | bytes 256 | tf_op jit(solution)/shard_map/psum | solution.py:67
  89.9 0.0 reduce-scatter.2.cloned.1.call-done
  89.9 0.0 copy-done.3
  89.9 1.8 %fusion.10 = bf16[128,256]{1,0:T(8,128)(2,1)} fusion(f32[128,256]{1,0:T(8,128)} %reduce-scatter.2.cloned.1.call-done, f32[4,256]{1,0:T(4,128)S(1)} %copy-done.3, s32[128]{0:T(128)S(1)} %convert_reduce_fusion), kind=kOutput, calls=%fused_computation.15 | convolution fusion | flops 1638912 | bytes 201216 | tf_op jit(solution)/shard_map/dot_general | solution.py:64
  (2 shorter events, 0.0 us)
Async XLA Ops:
  7.2 8.6 %copy-start = (bf16[1024,512]{1,0:T(8,128)(2,1)S(1)}, bf16[1024,512]{1,0:T(8,128)(2,1)}, u32[]{:S(2)}) copy-start(bf16[1024,512]{1,0:T(8,128)(2,1)} %param.10) | copy-start | bytes 3145732
  7.2 12.5 %copy-start.1 = (bf16[1,8,128,128]{3,2,1,0:T(8,128)(2,1)S(1)}, bf16[1,8,128,128]{3,2,1,0:T(8,128)(2,1)}, u32[]{:S(2)}) copy-start(bf16[1,8,128,128]{3,2,1,0:T(8,128)(2,1)} %param.11) | copy-start | bytes 786436
  7.2 19.1 %copy-start.2 = (bf16[128,256]{1,0:T(8,128)(2,1)S(1)}, bf16[128,256]{1,0:T(8,128)(2,1)}, u32[]{:S(2)}) copy-start(bf16[128,256]{1,0:T(8,128)(2,1)} %param.19) | copy-start | bytes 196612
  7.2 24.9 %copy-start.4 = (f32[1,32]{1,0:T(1,128)S(1)}, f32[1,32]{1,0:T(1,128)}, u32[]{:S(2)}) copy-start(f32[1,32]{1,0:T(1,128)} %param.15) | copy-start | bytes 388
  7.2 14.0 %all-to-all-start = ((s32[4,2,128]{2,1,0:T(2,128)}), s32[4,2,128]{2,1,0:T(2,128)S(1)}, u32[]{:S(2)}, u32[]{:S(2)}) async-start(s32[4,2,128]{2,1,0:T(2,128)} %bitcast.52), calls=%async_computation | async-start | bytes 8192 | tf_op jit(solution)/shard_map/all_to_all | solution.py:43
  21.2 30.3 %all-to-all-start.1 = ((bf16[8,128,512]{2,1,0:T(8,128)(2,1)}), bf16[8,128,512]{2,1,0:T(8,128)(2,1)S(1)}, u32[]{:S(2)}, u32[]{:S(2)}) async-start(bf16[8,128,512]{2,1,0:T(8,128)(2,1)} %convolution_convert_fusion), calls=%async_computation.1 | async-start | bytes 2097152 | tf_op jit(solution)/shard_map/all_to_all | solution.py:42
  26.3 27.1 %copy-start.5 = (s32[4]{0:T(128)S(1)}, s32[4]{0:T(128)}, u32[]{:S(2)}) copy-start(s32[4]{0:T(128)} %param.18) | copy-start | bytes 52
  26.3 63.6 %reduce-scatter.2.cloned.1.call-start = ((), (), s32[]{:S(2)}) async-start(), calls=%async_computation.3 | async-start | bytes 655360 | tf_op jit(solution)/shard_map/reduce_scatter | solution.py:57
  51.5 38.4 %copy-start.3 = (f32[4,256]{1,0:T(4,128)S(1)}, f32[4,256]{1,0:T(4,128)}, u32[]{:S(2)}) copy-start(f32[4,256]{1,0:T(4,128)} %param.17) | copy-start | bytes 12292
Sparse Core Ops, SparseCore 0:
  53.5 20.7 reduce-scatter.1
where the time goes:
time: 98.9 us; the launch traced here: 98.5 us
  matrix products  32.8 us (33%)
  blocking collectives  25.8 us (26%)
  between operations  14.1 us (14%)
  starting transfers between devices  11.6 us (12%)
  waiting for transfers between devices  7.93 us (8%)
  local copies, waits for them, and re-layouts  3.99 us (4%)
  other arithmetic  2.32 us (2%)
    psum x1, blocking collectives, on_device(): basis_grads = lax.psum(partial_value, ('dst', 'mp'))  20 us
    dot_general x1, matrix products, on_device(): jnp.dot(basis_flat, outer_sum.reshape(-1), precision=highest)  14.9 us
    dot_general x1, matrix products, on_device(): mixing = jnp.dot(basis_coef[0], basis_flat, precision=highest)  11.5 us
    all_to_all x1, waiting for transfers between devices, on_device(): lax.all_to_all(messages, 'dst', split_axis=0, concat_axis=0, tiled=True)  7.91 us
    all_to_all x1, starting transfers between devices, on_device(): lax.all_to_all(slot_local, 'dst', split_axis=0, concat_axis=0, tiled=True)  6.49 us
    all_gather x1, blocking collectives, on_device(): owner_grad = lax.all_gather(cotangent, 'rel', axis=0, tiled=True)  5.78 us
    all_to_all x1, starting transfers between devices, on_device(): lax.all_to_all(messages, 'dst', split_axis=0, concat_axis=0, tiled=True)  5.09 us
    gather x1, local copies, waits for them, and re-layouts, on_device(): jnp.take(node_table, src_ids[0].reshape(-1), axis=0)  3.96 us
  transfers between devices with their start and end apart: 3, of which 1 were waited for; matrix products, arithmetic and copies ran while one was open for 36% of the time, Pallas kernels for 0%

commit v1 on v0

--- a/solution.py
+++ b/solution.py
@@ -64,7 +64,8 @@
     row_bias = jnp.dot(kind_table, type_bias, precision=highest)
     layer_out = (relation_total + row_bias).astype(jnp.bfloat16)
     partial_value = jnp.dot(basis_flat, outer_sum.reshape(-1), precision=highest)
-    basis_grads = lax.psum(partial_value, ("dst", "mp"))
+    partial = lax.psum(partial_value, "mp")
+    basis_grads = lax.psum(partial, "dst")
     return (layer_out, basis_grads[None, :])
 
 

time: 98.9 us -> 93.9 us (0.949)
  blocking collectives: 25.8 us -> 21 us
    psum x1 -> x2, blocking collectives: 20 us -> 15.2 us  [the longest x1 10.3 us: on_device(): basis_grads = lax.psum(partial, 'dst')]
  transfers between devices with their start and end apart: 3 -> 3, of which waited for: 1 -> 1; matrix products, arithmetic and copies ran while one was open for 36% -> 38% of each run, Pallas kernels for 0% -> 0%
where the time goes in v1:
time: 93.9 us; the launch traced here: 93.5 us
  matrix products  32.8 us (35%)
  blocking collectives  21 us (22%)
  between operations  14.1 us (15%)
  starting transfers between devices  11.6 us (12%)
  waiting for transfers between devices  7.78 us (8%)
  local copies, waits for them, and re-layouts  3.99 us (4%)
  other arithmetic  2.32 us (2%)
    dot_general x1, matrix products, on_device(): jnp.dot(basis_flat, outer_sum.reshape(-1), precision=highest)  14.9 us
    dot_general x1, matrix products, on_device(): mixing = jnp.dot(basis_coef[0], basis_flat, precision=highest)  11.5 us
    psum x1, blocking collectives, on_device(): basis_grads = lax.psum(partial, 'dst')  10.3 us
    all_to_all x1, waiting for transfers between devices, on_device(): lax.all_to_all(messages, 'dst', split_axis=0, concat_axis=0, tiled=True)  7.76 us
    all_to_all x1, starting transfers between devices, on_device(): lax.all_to_all(slot_local, 'dst', split_axis=0, concat_axis=0, tiled=True)  6.49 us
    all_gather x1, blocking collectives, on_device(): owner_grad = lax.all_gather(cotangent, 'rel', axis=0, tiled=True)  5.76 us
    all_to_all x1, starting transfers between devices, on_device(): lax.all_to_all(messages, 'dst', split_axis=0, concat_axis=0, tiled=True)  5.09 us
    psum x1, blocking collectives, on_device(): partial = lax.psum(partial_value, 'mp')  4.93 us
  transfers between devices with their start and end apart: 3, of which 1 were waited for; matrix products, arithmetic and copies ran while one was open for 38% of the time, Pallas kernels for 0%

profile of v1, /device:TPU:0, one launch (start us, length us, event | category | flops | bytes accessed | tf_op | source)
XLA Modules:
  0.0 93.5 jit_solution(17576689547171174921)
XLA Ops:
  7.2 0.0 copy-start
  7.2 0.0 copy-start.1
  7.2 0.0 copy-start.4
  7.2 0.0 copy-start.2
  7.2 0.0 copy-start.5
  7.2 6.5 %all-to-all-start = ((s32[4,2,128]{2,1,0:T(2,128)}), s32[4,2,128]{2,1,0:T(2,128)S(1)}, u32[]{:S(2)}, u32[]{:S(2)}) async-start(s32[4,2,128]{2,1,0:T(2,128)} %bitcast.51), calls=%async_computation | async-start | bytes 8192 | tf_op jit(solution)/shard_map/all_to_all | solution.py:43
  13.7 0.7 compare_and_fusion
  14.4 0.7 compare_select_fusion
  15.1 0.7 convert_bitcast_fusion
  15.8 0.0 copy-done
  15.8 4.0 %gather_fusion = bf16[1024,512]{1,0:T(8,128)(2,1)S(1)} fusion(bf16[1024,512]{1,0:T(8,128)(2,1)S(1)} %copy-done, s32[1024]{0:T(1024)S(1)} %broadcast_clamp_fusion), kind=kCustom, calls=%fused_computation | custom fusion | bytes 2101248 | tf_op jit(solution)/shard_map/jit(_take)/gather | solution.py:29
  19.7 0.0 copy-done.1
  19.7 1.5 %convolution_convert_fusion = bf16[8,128,512]{2,1,0:T(8,128)(2,1)} fusion(bf16[8,128,512]{2,1,0:T(8,128)(2,1)S(1)} %bitcast.46, pred[8,128]{1,0:T(8,128)(4,1)S(1)} %compare_and_fusion, bf16[1,8,128,128]{3,2,1,0:T(8,128)(2,1)S(1)} %copy-done.1, bf16[8]{0:T(256)(128)(2,1)S(1)} %convert_bitcast_fusion), kind=kOutput, calls=%fused_computation.9 | convolution fusion | flops 135397376 | bytes 2360336 | tf_op jit(solution)/shard_map/kij,kjf->kif/dot_general | solution.py:33
  21.2 0.0 all-to-all-done
  21.2 5.1 %all-to-all-start.1 = ((bf16[8,128,512]{2,1,0:T(8,128)(2,1)}), bf16[8,128,512]{2,1,0:T(8,128)(2,1)S(1)}, u32[]{:S(2)}, u32[]{:S(2)}) async-start(bf16[8,128,512]{2,1,0:T(8,128)(2,1)} %convolution_convert_fusion), calls=%async_computation.1 | async-start | bytes 2097152 | tf_op jit(solution)/shard_map/all_to_all | solution.py:42
  26.3 0.0 reduce-scatter.2.cloned.1.call-start
  26.3 0.0 copy-done.4
  26.3 0.2 reduce-window.8
  26.5 0.0 copy-done.2
  26.5 5.8 %all_gather.3 = bf16[512,256]{1,0:T(8,128)(2,1)S(1)} all-gather(bf16[128,256]{1,0:T(8,128)(2,1)S(1)} %copy-done.2), channel_id=1, replica_groups=mesh['rel'=4,'dst'=4,'mp'=2] {'rel'}, dimensions={0}, use_global_device_ids=true | all-gather | bytes 327680 | tf_op jit(solution)/shard_map/all_gather | solution.py:39
  32.3 0.0 copy-done.5
  32.3 11.5 %fusion = bf16[1,512,256]{2,0,1:T(2,128)(2,1)S(1)} fusion(f32[1,32]{1,0:T(1,128)S(1)} %copy-done.5, bf16[4,8,512,256]{3,2,1,0:T(8,128)(2,1)} %bitcast.54), kind=kOutput, calls=%fused_computation.1 | convolution fusion | flops 50331648 | bytes 8650880 | tf_op jit(solution)/shard_map/dot_general | solution.py:37
  43.7 7.8 %all-to-all-done.1 = bf16[8,128,512]{2,1,0:T(8,128)(2,1)S(1)} async-done(((bf16[8,128,512]{2,1,0:T(8,128)(2,1)}), bf16[8,128,512]{2,1,0:T(8,128)(2,1)S(1)}, u32[]{:S(2)}, u32[]{:S(2)}) %all-to-all-start.1) | async-done | bytes 1048608 | tf_op jit(solution)/shard_map/all_to_all | solution.py:42
  51.5 0.0 copy-start.3
  51.5 1.9 %fusion.6 = f32[512,256]{1,0:T(8,128)} fusion(bf16[1024,512]{1,0:T(8,128)(2,1)S(1)} %bitcast.47, s32[1024]{0:T(1024)S(1)} %bitcast.52, bf16[1,512,256]{2,0,1:T(2,128)(2,1)S(1)} %fusion), kind=kOutput, calls=%fused_computation.8 | convolution fusion | flops 537657344 | bytes 1839104 | tf_op jit(solution)/shard_map/dot_general | solution.py:50
  53.4 0.0 reduce-scatter.2.cloned.1.call-update
  53.5 0.1 convert_reduce_fusion
  53.6 1.2 %fusion.9 = f32[512,256,1]{1,0,2:T(8,128)S(1)} fusion(bf16[1024,512]{1,0:T(8,128)(2,1)S(1)} %bitcast.48, bf16[512,256]{1,0:T(8,128)(2,1)S(1)} %all_gather.3, s32[1024]{0:T(1024)S(1)} %bitcast.53), kind=kOutput, calls=%fused_computation.13 | convolution fusion | flops 537657344 | bytes 1839104 | tf_op jit(solution)/shard_map/dot_general | solution.py:54
  54.8 14.9 %fusion.11 = f32[32]{0:T(128)S(1)} fusion(bf16[32,512,256]{2,1,0:T(8,128)(2,1)} %param.16, f32[512,256,1]{1,0,2:T(8,128)S(1)} %fusion.9), kind=kOutput, calls=%fused_computation.16 | convolution fusion | flops 50331648 | bytes 8913024 | tf_op jit(solution)/shard_map/dot_general | solution.py:66
  69.7 4.9 %psum.14 = f32[32]{0:T(128)S(1)} all-reduce(f32[32]{0:T(128)S(1)} %fusion.11), channel_id=1, replica_groups=mesh['rel'=4,'dst'=4,'mp'=2] {'mp'}, use_global_device_ids=true, to_apply=%region_3.4 | all-reduce | flops 32 | bytes 256 | tf_op jit(solution)/shard_map/psum | solution.py:67
  74.6 10.3 %psum.15 = f32[1,32]{1,0:T(1,128)} all-reduce(f32[1,32]{1,0:T(1,128)S(1)} %bitcast.57), channel_id=1, replica_groups=mesh['rel'=4,'dst'=4,'mp'=2] {'dst'}, use_global_device_ids=true, to_apply=%region_4.5 | all-reduce | flops 32 | bytes 256 | tf_op jit(solution)/shard_map/psum | solution.py:68
  84.9 0.0 reduce-scatter.2.cloned.1.call-done
  84.9 0.0 copy-done.3
  84.9 1.8 %fusion.10 = bf16[128,256]{1,0:T(8,128)(2,1)} fusion(f32[128,256]{1,0:T(8,128)} %reduce-scatter.2.cloned.1.call-done, f32[4,256]{1,0:T(4,128)S(1)} %copy-done.3, s32[128]{0:T(128)S(1)} %convert_reduce_fusion), kind=kOutput, calls=%fused_computation.15 | convolution fusion | flops 1638912 | bytes 201216 | tf_op jit(solution)/shard_map/dot_general | solution.py:64
  (2 shorter events, 0.0 us)
Async XLA Ops:
  7.2 8.6 %copy-start = (bf16[1024,512]{1,0:T(8,128)(2,1)S(1)}, bf16[1024,512]{1,0:T(8,128)(2,1)}, u32[]{:S(2)}) copy-start(bf16[1024,512]{1,0:T(8,128)(2,1)} %param.10) | copy-start | bytes 3145732
  7.2 12.6 %copy-start.1 = (bf16[1,8,128,128]{3,2,1,0:T(8,128)(2,1)S(1)}, bf16[1,8,128,128]{3,2,1,0:T(8,128)(2,1)}, u32[]{:S(2)}) copy-start(bf16[1,8,128,128]{3,2,1,0:T(8,128)(2,1)} %param.11) | copy-start | bytes 786436
  7.2 19.1 %copy-start.4 = (s32[4]{0:T(128)S(1)}, s32[4]{0:T(128)}, u32[]{:S(2)}) copy-start(s32[4]{0:T(128)} %param.18) | copy-start | bytes 52
  7.2 19.3 %copy-start.2 = (bf16[128,256]{1,0:T(8,128)(2,1)S(1)}, bf16[128,256]{1,0:T(8,128)(2,1)}, u32[]{:S(2)}) copy-start(bf16[128,256]{1,0:T(8,128)(2,1)} %param.19) | copy-start | bytes 196612
  7.2 25.1 %copy-start.5 = (f32[1,32]{1,0:T(1,128)S(1)}, f32[1,32]{1,0:T(1,128)}, u32[]{:S(2)}) copy-start(f32[1,32]{1,0:T(1,128)} %param.15) | copy-start | bytes 388
  7.2 14.0 %all-to-all-start = ((s32[4,2,128]{2,1,0:T(2,128)}), s32[4,2,128]{2,1,0:T(2,128)S(1)}, u32[]{:S(2)}, u32[]{:S(2)}) async-start(s32[4,2,128]{2,1,0:T(2,128)} %bitcast.51), calls=%async_computation | async-start | bytes 8192 | tf_op jit(solution)/shard_map/all_to_all | solution.py:43
  21.2 30.3 %all-to-all-start.1 = ((bf16[8,128,512]{2,1,0:T(8,128)(2,1)}), bf16[8,128,512]{2,1,0:T(8,128)(2,1)S(1)}, u32[]{:S(2)}, u32[]{:S(2)}) async-start(bf16[8,128,512]{2,1,0:T(8,128)(2,1)} %convolution_convert_fusion), calls=%async_computation.1 | async-start | bytes 2097152 | tf_op jit(solution)/shard_map/all_to_all | solution.py:42
  26.3 58.6 %reduce-scatter.2.cloned.1.call-start = ((), (), s32[]{:S(2)}) async-start(), calls=%async_computation.3 | async-start | bytes 655360 | tf_op jit(solution)/shard_map/reduce_scatter | solution.py:57
  51.5 33.4 %copy-start.3 = (f32[4,256]{1,0:T(4,128)S(1)}, f32[4,256]{1,0:T(4,128)}, u32[]{:S(2)}) copy-start(f32[4,256]{1,0:T(4,128)} %param.17) | copy-start | bytes 12292
Sparse Core Ops, SparseCore 0:
  53.6 20.7 reduce-scatter.1
